TPU v7x, 32 devices: a whole 2x2x4 slice. The times are simulated.
32 devices in a mesh: rep: 4 (over x, core), fsdp: 8 (over z, y).
Axes of the slice: x: 2, y: 2, z: 4, core: 2. Of those that a mesh axis runs over, the one named last changes fastest.
Arguments:
- tokens: bfloat16 [32768, 1024], P(('rep', 'fsdp')), may hold values from -6 to 6
- cotangent: bfloat16 [32768, 1024], P(('rep', 'fsdp')), may hold values from -6 to 6
- segment_ids: int32 [32, 1024], P(('rep', 'fsdp')), may hold values from 0 to 15, never falling along the last dimension, each value on 1 to 512 neighbouring positions
- attention_weight: float32 [4, 1024, 1024], P(None, 'fsdp'), may hold values from -0.375 to 0.375
- attention_momentum: float32 [4, 1024, 1024], P(None, 'fsdp'), may hold values from -0.1875 to 0.1875
- attention_first: float32 [4, 4, 1024, 1024], P('rep', None, 'fsdp'), may hold values from -112 to 112
- attention_second: float32 [4, 4, 1024, 1024], P('rep', None, 'fsdp'), may hold values from 54.8864 to 876.544
- expand_weight: float32 [1024, 4096], P('fsdp'), may hold values from -0.1875 to 0.1875
- expand_momentum: float32 [1024, 4096], P('fsdp'), may hold values from -0.1875 to 0.1875
- expand_first: float32 [4, 1024, 4096], P('rep', 'fsdp'), may hold values from -128 to 128
- expand_second: float32 [4, 1024, 4096], P('rep', 'fsdp'), may hold values from 85.1968 to 1368.064
- contract_weight: float32 [4096, 1024], P('fsdp'), may hold values from -0.09375 to 0.09375
- contract_momentum: float32 [4096, 1024], P('fsdp'), may hold values from -0.09375 to 0.09375
- contract_first: float32 [4, 4096, 1024], P('rep', 'fsdp'), may hold values from -256 to 256
- contract_second: float32 [4, 4096, 1024], P('rep', 'fsdp'), may hold values from 341.6064 to 5464.064
- vectors: float32 [12, 1024], P(None, 'fsdp'), may hold values from -0.6 to 1.4
- vectors_momentum: float32 [12, 1024], P(None, 'fsdp'), may hold values from -1.25 to 1.25
- vectors_first: float32 [4, 12, 1024], P('rep', None, 'fsdp'), may hold values from -448 to 448
- vectors_second: float32 [4, 12, 1024], P('rep', None, 'fsdp'), may hold values from 876.544 to 14008.32
Outputs:
- layer_output: bfloat16 [32768, 1024], P(('rep', 'fsdp'))
- input_grad: bfloat16 [32768, 1024], P(('rep', 'fsdp'))
- attention_first_new: float32 [4, 4, 1024, 1024], P('rep', None, 'fsdp')
- attention_second_new: float32 [4, 4, 1024, 1024], P('rep', None, 'fsdp')
- outer_attention: float32 [3, 4, 1024, 1024], P(None, None, 'fsdp')
- copy_attention: bfloat16 [4, 1024, 1024], P(None, 'fsdp')
- expand_first_new: float32 [4, 1024, 4096], P('rep', 'fsdp')
- expand_second_new: float32 [4, 1024, 4096], P('rep', 'fsdp')
- outer_expand: float32 [3, 1024, 4096], P(None, 'fsdp')
- copy_expand: bfloat16 [1024, 4096], P('fsdp')
- contract_first_new: float32 [4, 4096, 1024], P('rep', 'fsdp')
- contract_second_new: float32 [4, 4096, 1024], P('rep', 'fsdp')
- outer_contract: float32 [3, 4096, 1024], P(None, 'fsdp')
- copy_contract: bfloat16 [4096, 1024], P('fsdp')
- vectors_first_new: float32 [4, 12, 1024], P('rep', None, 'fsdp')
- vectors_second_new: float32 [4, 12, 1024], P('rep', None, 'fsdp')
- outer_vectors: float32 [3, 12, 1024], P(None, None, 'fsdp')
- copy_vectors: bfloat16 [12, 1024], P(None, 'fsdp')
Inputs may be any that keep to these rules, and one draw needn't show every extreme that they name: `segment_ids`: within a row the numbers never fall; a run of equal numbers is one document, and tokens attend only within their document.
All inputs are finite; a program needn't handle non-finite values.
Results may differ from a plain program's by a relative error of at most 0.012.
The roundings to bfloat16 on the way count: a program that leaves them out, or rounds other values in their place, can miss the bound.
Values may be sent and summed in bfloat16 or wider, within the bound.
A program may use at most 448 MiB of HBM per device.

v0:
```python
from functools import partial
import jax
import jax.numpy as jnp
from jax import lax
from jax.sharding import PartitionSpec as P

D = 1024
H = 16
HD = 64
FF = 4096
LEN = 1024
SEQ_DEV = 1
ADAM_STEP = 4
TOK_DEV = 1024


def norm_forward(values_in, gain_row, shift_row):
    center = values_in - jnp.mean(values_in, axis=-1, keepdims=True)
    inv_scale = lax.rsqrt(jnp.mean(center * center, axis=-1, keepdims=True) + 1e-05)
    normed = center * inv_scale
    return (normed * gain_row + shift_row, normed, inv_scale)


def norm_backward(grad_out, normed, inv_scale, gain_row):
    grad_gain = jnp.sum(grad_out * normed, axis=0)
    grad_shift = jnp.sum(grad_out, axis=0)
    scaled_grad = grad_out * gain_row
    grad_value = inv_scale * (
        scaled_grad
        - jnp.mean(scaled_grad, axis=-1, keepdims=True)
        - normed * jnp.mean(scaled_grad * normed, axis=-1, keepdims=True)
    )
    return (grad_value, grad_gain, grad_shift)


def product_over(left, right):
    return lax.dot_general(
        left, right, (((0,), (0,)), ((), ())), preferred_element_type=jnp.float32
    )


def product_back(left, right):
    return lax.dot_general(
        left, right, (((1,), (1,)), ((), ())), preferred_element_type=jnp.float32
    )


def block_scores(query_block, key_block, row_segments, all_segments):
    scores = jnp.einsum("qhd,khd->hqk", query_block, key_block, preferred_element_type=jnp.float32)
    same_doc = row_segments[:, None] == all_segments[None, :]
    return jnp.where(same_doc[None], scores, -1e30)


def inner_step(weight, gradient, first_moment, second_moment, learn_rate, weight_decay):
    first_new = 0.5 * first_moment + 0.5 * gradient
    second_new = 0.75 * second_moment + 0.25 * gradient * gradient
    update_dir = (
        first_new
        / (1.0 - 0.5**ADAM_STEP)
        / (jnp.sqrt(second_new / (1.0 - 0.75**ADAM_STEP)) + 1e-08)
    )
    return (weight - learn_rate * (update_dir + weight_decay * weight), first_new, second_new)


def per_device(
    tokens,
    cotangent,
    segment_ids,
    attention_weight,
    attention_momentum,
    attention_first,
    attention_second,
    expand_weight,
    expand_momentum,
    expand_first,
    expand_second,
    contract_weight,
    contract_momentum,
    contract_first,
    contract_second,
    vectors,
    vectors_momentum,
    vectors_first,
    vectors_second,
):
    attn_full, vector_full = (
        lax.all_gather(attention_weight.astype(jnp.bfloat16), "fsdp", axis=1, tiled=True),
        lax.all_gather(vectors.astype(jnp.bfloat16), "fsdp", axis=1, tiled=True),
    )
    vector_rows = vector_full.astype(jnp.float32)
    gain_one, gain_two, shift_one, shift_two = (
        vector_rows[0],
        vector_rows[1],
        vector_rows[2],
        vector_rows[3],
    )
    bias_query, bias_value, bias_mixed, bias_down = (
        vector_rows[4],
        vector_rows[5],
        vector_rows[6],
        vector_rows[7],
    )
    bias_up = vector_rows[8:].reshape(FF)
    projected = jnp.einsum("td,nde->nte", tokens, attn_full[:3], preferred_element_type=jnp.float32)
    query_all = ((projected[0] + bias_query) * 0.125).astype(jnp.bfloat16)
    key_all = projected[1].astype(jnp.bfloat16)
    value_all = (projected[2] + bias_value).astype(jnp.bfloat16)
    query_heads = query_all.reshape(SEQ_DEV, LEN, H, HD)
    key_heads = key_all.reshape(SEQ_DEV, LEN, H, HD)
    value_heads = value_all.reshape(SEQ_DEV, LEN, H, HD)
    block_rows = min(512, LEN)
    head_group = min(8, H)
    context_rows = []
    log_sums = []
    seq_index = 0
    for row_start in range(0, LEN, block_rows):
        block_pieces = []
        for head_start in range(0, H, head_group):
            head_part = slice(head_start, head_start + head_group)
            scores = block_scores(
                query_heads[seq_index, row_start : row_start + block_rows, head_part],
                key_heads[seq_index, :, head_part],
                segment_ids[seq_index, row_start : row_start + block_rows],
                segment_ids[seq_index],
            )
            row_max = jnp.max(scores, axis=-1, keepdims=True)
            exp_score = jnp.exp(scores - row_max)
            row_total = jnp.sum(exp_score, axis=-1, keepdims=True)
            probability = (exp_score / row_total).astype(jnp.bfloat16)
            block_pieces.append(
                jnp.einsum(
                    "hqk,khd->qhd",
                    probability,
                    value_heads[seq_index, :, head_part],
                    preferred_element_type=jnp.float32,
                )
            )
            log_sums.append(row_max + jnp.log(row_total))
        context_rows.append(jnp.concatenate(block_pieces, axis=1))
    mixed = jnp.concatenate(context_rows, axis=0).reshape(TOK_DEV, D).astype(jnp.bfloat16)
    attn_out = jnp.dot(mixed, attn_full[3], preferred_element_type=jnp.float32) + bias_mixed
    hidden, normed_one, scale_one = norm_forward(
        tokens.astype(jnp.float32) + attn_out, gain_one, shift_one
    )
    hidden_low = hidden.astype(jnp.bfloat16)
    ffn_expand, ffn_contract = (
        lax.all_gather(expand_weight.astype(jnp.bfloat16), "fsdp", axis=0, tiled=True),
        lax.all_gather(contract_weight.astype(jnp.bfloat16), "fsdp", axis=0, tiled=True),
    )
    pre_act = jnp.dot(hidden_low, ffn_expand, preferred_element_type=jnp.float32) + bias_up
    activated = jax.nn.gelu(pre_act, approximate=False).astype(jnp.bfloat16)
    branch = jnp.dot(activated, ffn_contract, preferred_element_type=jnp.float32) + bias_down
    layer_output, normed_two, scale_two = norm_forward(hidden + branch, gain_two, shift_two)
    grad_sum, grad_gain_two, grad_shift_two = norm_backward(
        cotangent.astype(jnp.float32), normed_two, scale_two, gain_two
    )
    grad_branch = grad_sum.astype(jnp.bfloat16)
    grad_act = product_back(grad_branch, ffn_contract)
    unused_value, gelu_pull = jax.vjp(partial(jax.nn.gelu, approximate=False), pre_act)
    grad_pre_low = gelu_pull(grad_act)[0].astype(jnp.bfloat16)
    grad_hidden = grad_sum + product_back(grad_pre_low, ffn_expand)
    contract_full = product_over(activated, grad_branch)
    expand_full = product_over(hidden_low, grad_pre_low)
    grad_expand, grad_contract = (
        lax.psum_scatter(expand_full, "fsdp", scatter_dimension=0, tiled=True),
        lax.psum_scatter(contract_full, "fsdp", scatter_dimension=0, tiled=True),
    )
    grad_resid, grad_gain_one, grad_shift_one = norm_backward(
        grad_hidden, normed_one, scale_one, gain_one
    )
    grad_attn_out = grad_resid.astype(jnp.bfloat16)
    grad_bias_mixed = jnp.sum(grad_attn_out.astype(jnp.float32), axis=0)
    grad_output_proj = product_over(mixed, grad_attn_out)
    grad_mixed = product_back(grad_attn_out, attn_full[3]).astype(jnp.bfloat16)
    grad_context = grad_mixed.reshape(SEQ_DEV, LEN, H, HD)
    query_grads = []
    lse_index = 0
    seq_index = 0
    key_totals = [
        jnp.zeros((LEN, head_group, HD), jnp.float32) for head_start in range(0, H, head_group)
    ]
    value_totals = [
        jnp.zeros((LEN, head_group, HD), jnp.float32) for head_start in range(0, H, head_group)
    ]
    for row_start in range(0, LEN, block_rows):
        block_pieces = []
        for group_index, head_start in enumerate(range(0, H, head_group)):
            head_part = slice(head_start, head_start + head_group)
            query_block = query_heads[seq_index, row_start : row_start + block_rows, head_part]
            key_block = key_heads[seq_index, :, head_part]
            value_block = value_heads[seq_index, :, head_part]
            ctx_grad = grad_context[seq_index, row_start : row_start + block_rows, head_part]
            scores = block_scores(
                query_block,
                key_block,
                segment_ids[seq_index, row_start : row_start + block_rows],
                segment_ids[seq_index],
            )
            probability = jnp.exp(scores - log_sums[lse_index])
            lse_index = lse_index + 1
            value_totals[group_index] = value_totals[group_index] + jnp.einsum(
                "hqk,qhd->khd",
                probability.astype(jnp.bfloat16),
                ctx_grad,
                preferred_element_type=jnp.float32,
            )
            prob_grad = jnp.einsum(
                "qhd,khd->hqk", ctx_grad, value_block, preferred_element_type=jnp.float32
            )
            row_dot = jnp.sum(probability * prob_grad, axis=-1, keepdims=True)
            score_grad = (probability * (prob_grad - row_dot)).astype(jnp.bfloat16)
            block_pieces.append(
                jnp.einsum(
                    "hqk,khd->qhd", score_grad, key_block, preferred_element_type=jnp.float32
                ).astype(jnp.bfloat16)
            )
            key_totals[group_index] = key_totals[group_index] + jnp.einsum(
                "hqk,qhd->khd", score_grad, query_block, preferred_element_type=jnp.float32
            )
        query_grads.append(jnp.concatenate(block_pieces, axis=1))
    key_grads = jnp.concatenate(
        [key_total.astype(jnp.bfloat16) for key_total in key_totals], axis=1
    )
    value_grads = jnp.concatenate(
        [value_total.astype(jnp.bfloat16) for value_total in value_totals], axis=1
    )
    grad_query = jnp.concatenate(query_grads, axis=0).reshape(TOK_DEV, D) * 0.125
    grad_keys = key_grads.reshape(TOK_DEV, D)
    grad_values = value_grads.reshape(TOK_DEV, D)
    stacked_grads = jnp.stack([grad_query, grad_keys, grad_values])
    grad_qkv = jnp.einsum("td,nte->nde", tokens, stacked_grads, preferred_element_type=jnp.float32)
    input_grad = (
        grad_resid
        + jnp.einsum(
            "nte,nde->td", stacked_grads, attn_full[:3], preferred_element_type=jnp.float32
        )
    ).astype(jnp.bfloat16)
    grad_attention_full = jnp.concatenate([grad_qkv, grad_output_proj[None]], axis=0)
    vector_head = jnp.stack(
        [
            grad_gain_one,
            grad_gain_two,
            grad_shift_one,
            grad_shift_two,
            jnp.sum(grad_query.astype(jnp.float32), axis=0),
            jnp.sum(grad_values.astype(jnp.float32), axis=0),
            grad_bias_mixed,
            jnp.sum(grad_branch.astype(jnp.float32), axis=0),
        ]
    )
    grad_bias_up = jnp.sum(grad_pre_low.astype(jnp.float32), axis=0).reshape(FF // D, D)
    grad_vectors_full = jnp.concatenate([vector_head, grad_bias_up], axis=0)
    grad_attention, grad_vectors = (
        lax.psum_scatter(grad_attention_full, "fsdp", scatter_dimension=1, tiled=True),
        lax.psum_scatter(grad_vectors_full, "fsdp", scatter_dimension=1, tiled=True),
    )
    attention_new = inner_step(
        attention_weight, grad_attention, attention_first[0], attention_second[0], 0.03, 0.1
    )
    expand_new = inner_step(
        expand_weight, grad_expand, expand_first[0], expand_second[0], 0.03, 0.1
    )
    contract_new = inner_step(
        contract_weight, grad_contract, contract_first[0], contract_second[0], 0.015, 0.1
    )
    vectors_new = inner_step(vectors, grad_vectors, vectors_first[0], vectors_second[0], 0.2, 0.0)
    summed = (
        lax.psum((attention_weight - attention_new[0]).astype(jnp.bfloat16), "rep").astype(
            jnp.float32
        ),
        lax.psum((expand_weight - expand_new[0]).astype(jnp.bfloat16), "rep").astype(jnp.float32),
        lax.psum((contract_weight - contract_new[0]).astype(jnp.bfloat16), "rep").astype(
            jnp.float32
        ),
        lax.psum((vectors - vectors_new[0]).astype(jnp.bfloat16), "rep").astype(jnp.float32),
    )
    groups_count = lax.axis_size("rep")
    results = []
    for weight_now, momentum_now, inner_new, diff_total in zip(
        (attention_weight, expand_weight, contract_weight, vectors),
        (attention_momentum, expand_momentum, contract_momentum, vectors_momentum),
        (attention_new, expand_new, contract_new, vectors_new),
        summed,
    ):
        mean_diff = diff_total / groups_count
        momentum_new = 0.5 * momentum_now + mean_diff
        outer_new = weight_now - 0.7 * (mean_diff + 0.5 * momentum_new)
        results.append(
            (
                inner_new[1][None],
                inner_new[2][None],
                jnp.stack([mean_diff, momentum_new, outer_new]),
                outer_new.astype(jnp.bfloat16),
            )
        )
    return (
        layer_output.astype(jnp.bfloat16),
        input_grad,
        results[0][0],
        results[0][1],
        results[0][2],
        results[0][3],
        results[1][0],
        results[1][1],
        results[1][2],
        results[1][3],
        results[2][0],
        results[2][1],
        results[2][2],
        results[2][3],
        results[3][0],
        results[3][1],
        results[3][2],
        results[3][3],
    )


def solution(mesh):
    placed = (
        P(("rep", "fsdp"), None),
        P(("rep", "fsdp"), None),
        P(("rep", "fsdp"), None),
        P(None, "fsdp", None),
        P(None, "fsdp", None),
        P("rep", None, "fsdp", None),
        P("rep", None, "fsdp", None),
        P("fsdp", None),
        P("fsdp", None),
        P("rep", "fsdp", None),
        P("rep", "fsdp", None),
        P("fsdp", None),
        P("fsdp", None),
        P("rep", "fsdp", None),
        P("rep", "fsdp", None),
        P(None, "fsdp"),
        P(None, "fsdp"),
        P("rep", None, "fsdp"),
        P("rep", None, "fsdp"),
    )
    return jax.shard_map(
        per_device,
        mesh=mesh,
        in_specs=placed,
        out_specs=(
            P(("rep", "fsdp"), None),
            P(("rep", "fsdp"), None),
            P("rep", None, "fsdp", None),
            P("rep", None, "fsdp", None),
            P(None, None, "fsdp", None),
            P(None, "fsdp", None),
            P("rep", "fsdp", None),
            P("rep", "fsdp", None),
            P(None, "fsdp", None),
            P("fsdp", None),
            P("rep", "fsdp", None),
            P("rep", "fsdp", None),
            P(None, "fsdp", None),
            P("fsdp", None),
            P("rep", None, "fsdp"),
            P("rep", None, "fsdp"),
            P(None, None, "fsdp"),
            P(None, "fsdp"),
        ),
        check_vma=False,
    )
```

profile of v0, /device:TPU:0, one launch (start us, length us, event | category | flops | bytes accessed | tf_op | source)
XLA Modules:
  0.0 1465.5 jit_solution(9158751748262666368)
XLA Ops:
  16.3 28.9 %all_gather.13 = bf16[12,1024]{1,0:T(8,128)(2,1)S(1)} all-gather(bf16[12,128]{1,0:T(8,128)(2,1)S(1)} %convert_element_type.221), channel_id=1, replica_groups=mesh['rep'=4,'fsdp'=8] {'fsdp'}, dimensions={1}, use_global_device_ids=true | all-gather | bytes 27648 | tf_op jit(solution)/shard_map/all_gather | solution.py:88
  54.0 84.8 %all-gather.4.cloned.1.call-done = bf16[4,1024,1024]{1,2,0:T(8,128)(2,1)} async-done(((bf16[4,128,1024]{1,2,0:T(8,128)(2,1)}), bf16[4,1024,1024]{1,2,0:T(8,128)(2,1)}) %all-gather.4.cloned.1.call-update) | async-done | bytes 8388624 | tf_op jit(solution)/shard_map/all_gather | solution.py:87
  138.7 9.0 convolution_bitcast_fusion.1
  158.2 8.4 select_reduce_fusion.1
  166.6 8.4 select_reduce_fusion.3
  176.6 13.4 fusion.6
  190.0 8.9 fusion.7
  208.6 8.9 fusion.78
  217.6 13.5 fusion.8
  231.1 8.6 fusion.9
  247.1 8.3 fusion.76
  264.1 48.0 %multiply_convert_fusion.4 = (bf16[1024,4096]{1,0:T(8,128)(2,1)}, f32[1024,4096]{1,0:T(8,128)}, f32[1024,4096]{1,0:T(8,128)}) fusion(f32[4096]{0:T(1024)S(1)} %bitcast.308, bf16[1024,4096]{1,0:T(8,128)(2,1)} %all-gather.6.cloned.1.call-done, bf16[1024,1024]{0,1:T(8,128)(2,1)S(1)} %fusion.134.clone.4), kind=kOutput, calls=%fused_computation.17 | convolution fusion | flops 8866758656 | bytes 52445184 | tf_op jit(solution)/shard_map/dot_general | solution.py:150
  312.1 77.4 %all-gather.8.cloned.1.call-done = bf16[4096,1024]{1,0:T(8,128)(2,1)} async-done(((bf16[512,1024]{1,0:T(8,128)(2,1)}), bf16[4096,1024]{1,0:T(8,128)(2,1)}) %all-gather.8.cloned.1.call-update) | async-done | bytes 8388624 | tf_op jit(solution)/shard_map/all_gather | solution.py:148
  389.5 14.9 %fusion.141 = (f32[1024]{0:T(1024)S(1)}, f32[1024,1024]{0,1:T(8,128)S(1)}) fusion(f32[1024]{0:T(1024)S(1)} %bitcast.316, bf16[1024,4096]{1,0:T(8,128)(2,1)} %get-tuple-element.65, bf16[4096,1024]{1,0:T(8,128)(2,1)} %all-gather.8.cloned.1.call-done, f32[1024]{0:T(1024)S(1)} %bitcast.304, f32[1024]{0:T(1024)S(1)} %bitcast.294, ...), kind=kOutput, calls=%fused_computation.264 | convolution fusion | flops 8597273600 | bytes 25190400 | tf_op jit(solution)/shard_map/dot_general | solution.py:152
  414.7 24.3 %convert_reduce_fusion = (f32[4096]{0:T(1024)}, bf16[1024,4096]{1,0:T(8,128)(2,1)}) fusion(f32[1024,4096]{1,0:T(8,128)} %get-tuple-element.66, f32[1024,4096]{1,0:T(8,128)} %get-tuple-element.120, f32[4096]{0:T(1024)S(1)} %bitcast.309, bf16[1024,1024]{0,1:T(8,128)(2,1)} %get-tuple-element.60, bf16[4096,1024]{1,0:T(8,128)(2,1)} %all-gather.8.cloned.1.call-done), kind=kOutput, calls=%fused_computation.3 | convolution fusion | flops 8661233664 | bytes 52461568 | tf_op jit(solution)/shard_map/dot_general | solution.py:43
  439.0 14.9 %fusion.131 = f32[1024,4096]{1,0:T(8,128)} fusion(bf16[1024,4096]{1,0:T(8,128)(2,1)} %get-tuple-element.58, f32[1024,1024]{0,1:T(8,128)S(1)} %copy-done.7, f32[1024]{0:T(1024)S(1)} %bitcast.305, f32[1024]{0:T(1024)S(1)} %bitcast.295, f32[1024]{0:T(1024)S(1)} %add_rsqrt_fusion.1, f32[1024]{0:T(1024)S(1)} %broadcast_multiply_fusion.5), kind=kOutput, calls=%fused_computation.258 | convolution fusion | flops 8595177472 | bytes 29376512 | tf_op jit(solution)/shard_map/dot_general | solution.py:37
  455.5 19.6 %multiply_reduce_fusion.4 = (f32[1024]{0:T(1024)}, f32[1024]{0:T(1024)S(1)}, f32[1024]{0:T(1024)S(1)}, f32[1024]{0:T(1024)}, f32[1024,1024]{0,1:T(8,128)S(1)}) fusion(f32[1024,1024]{0,1:T(8,128)} %copy-done.6, f32[1024]{0:T(1024)S(1)} %add_rsqrt_fusion.1, f32[1024]{0:T(1024)S(1)} %broadcast_multiply_fusion.5, f32[1024]{0:T(1024)S(1)} %bitcast.296, ...), kind=kOutput, calls=%fused_computation.96 | convolution fusion | flops 8608804864 | bytes 31506432 | tf_op jit(solution)/shard_map/dot_general | solution.py:43
  483.0 9.9 fusion.14
  493.0 9.9 fusion.16
  509.7 10.6 fusion.81
  526.0 9.4 fusion.95
  535.5 9.3 fusion.96
  544.8 21.2 %multiply_reduce_fusion.3 = (f32[8,512]{1,0:T(8,128)}, f32[8,512]{1,0:T(8,128)}, f32[8,512,1024]{2,1,0:T(8,128)}) fusion(f32[8,512,1024]{2,1,0:T(8,128)} %get-tuple-element.116, f32[8,512]{1,0:T(8,128)} %copy-done.50, pred[512,1024]{1,0:T(8,128)(4,1)S(1)} %copy-done.11, f32[8,512,1024]{2,1,0:T(8,128)} %fusion.96, f32[8,512]{1,0:T(8,128)} %copy-done.52, ...), kind=kOutput, calls=%fused_computation.14 | convolution fusion | flops 570417152 | bytes 69271552 | tf_op jit(solution)/shard_map/qhd,khd->hqk/dot_general | solution.py:207
  566.1 24.3 %multiply_reduce_fusion.1 = (f32[8,512]{1,0:T(8,128)S(1)}, f32[8,512]{1,0:T(8,128)S(1)}, f32[8,512,1024]{2,1,0:T(8,128)}) fusion(f32[8,512,1024]{2,1,0:T(8,128)} %get-tuple-element.113, f32[8,512]{1,0:T(8,128)} %copy-done.54, pred[512,1024]{1,0:T(8,128)(4,1)S(1)} %copy-done.13, f32[8,512,1024]{2,1,0:T(8,128)} %fusion.95, f32[8,512]{1,0:T(8,128)} %copy-done.56, ...), kind=kOutput, calls=%fused_computation.8 | convolution fusion | flops 570417152 | bytes 69271552 | tf_op jit(solution)/shard_map/qhd,khd->hqk/dot_general | solution.py:207
  590.5 52.7 %multiply_convert_fusion.1 = (bf16[8,512,1024]{2,1,0:T(8,128)(2,1)}, bf16[8,512,1024]{2,1,0:T(8,128)(2,1)S(1)}, bf16[8,512,1024]{2,1,0:T(8,128)(2,1)}, bf16[8,512,1024]{2,1,0:T(8,128)(2,1)}) fusion(f32[8,512,1024]{2,1,0:T(8,128)} %get-tuple-element.125, f32[8,512,1024]{2,1,0:T(8,128)} %get-tuple-element.113, f32[8,512]{1,0:T(8,128)S(1)} %get-tuple-element.44, ...), kind=kLoop, calls=%fused_computation.7 | loop fusion | flops 83886080 | bytes 168951808 | tf_op jit(solution)/shard_map/convert_element_type | solution.py:211
  710.0 14.9 %fusion.142 = f32[4096,1024]{1,0:T(8,128)} fusion(bf16[1024,4096]{1,0:T(8,128)(2,1)} %get-tuple-element.65, bf16[1024,1024]{0,1:T(8,128)(2,1)S(1)} %copy-done.45), kind=kOutput, calls=%fused_computation.265 | convolution fusion | flops 8589934592 | bytes 27262976 | tf_op jit(solution)/shard_map/dot_general | solution.py:37
  740.4 8.5 fusion.100
  748.9 266.6 %reduce-scatter.5.cloned.1.call-done = f32[4,128,1024]{1,2,0:T(8,128)} async-done(((f32[4,1024,1024]{1,2,0:T(8,128)}), f32[4,128,1024]{1,2,0:T(8,128)}) %reduce-scatter.5.cloned.1.call-update) | async-done | bytes 2097168 | tf_op jit(solution)/shard_map/reduce_scatter | solution.py:254
  1021.7 276.8 %reduce-scatter.9.cloned.1.call-done = f32[512,1024]{1,0:T(8,128)} async-done(((f32[4096,1024]{1,0:T(8,128)}), f32[512,1024]{1,0:T(8,128)}) %reduce-scatter.9.cloned.1.call-update) | async-done | bytes 2097168 | tf_op jit(solution)/shard_map/reduce_scatter | solution.py:166
  1306.4 13.0 fusion.47
  1323.4 32.2 %reduce-scatter.11.cloned.1.call-done = f32[12,128]{1,0:T(8,128)} async-done(((f32[12,1024]{1,0:T(8,128)}), f32[12,128]{1,0:T(8,128)}) %reduce-scatter.11.cloned.1.call-update) | async-done | bytes 6160 | tf_op jit(solution)/shard_map/reduce_scatter | solution.py:255
  1370.4 56.4 %all-reduce.3.cloned.1.call-done = (bf16[4,128,1024]{1,2,0:T(8,128)(2,1)}, bf16[128,4096]{1,0:T(8,128)(2,1)}, bf16[512,1024]{1,0:T(8,128)(2,1)}) async-done(((bf16[4,128,1024]{1,2,0:T(8,128)(2,1)}, bf16[128,4096]{1,0:T(8,128)(2,1)}, bf16[512,1024]{1,0:T(8,128)(2,1)}), (bf16[4,128,1024]{1,2,0:T(8,128)(2,1)}, bf16[128,4096]{1,0:T(8,128)(2,1)}, bf16[512,1024]{1,0:T(8,128)(2,1)})) %all-reduce.3.cloned.1.call-update) | async-done | bytes 3145744 | tf_op jit(solution)/shard_map/psum | solution.py:268
  (329 shorter events, 233.4 us)
Async XLA Ops:
  7.2 131.6 %all-gather.4.cloned.1.call-start = ((), (), s32[]{:S(2)}) async-start(), calls=%async_computation.4 | async-start | bytes 9437184 | tf_op jit(solution)/shard_map/all_gather | solution.py:87
  10.5 35.4 %copy-start.84 = (s32[1,1024]{1,0:T(1,128)S(1)}, s32[1,1024]{1,0:T(1,128)}, u32[]{:S(2)}) copy-start(s32[1,1024]{1,0:T(1,128)} %param.21) | copy-start | bytes 12292
  10.5 253.7 %all-gather.6.cloned.1.call-start = ((), (), s32[]{:S(2)}) async-start(), calls=%async_computation.5 | async-start | bytes 9437184 | tf_op jit(solution)/shard_map/all_gather | solution.py:147
  13.3 376.3 %all-gather.8.cloned.1.call-start = ((), (), s32[]{:S(2)}) async-start(), calls=%async_computation.6 | async-start | bytes 9437184 | tf_op jit(solution)/shard_map/all_gather | solution.py:148
  13.3 33.4 %copy-start.36 = (bf16[1024,1024]{1,0:T(8,128)(2,1)S(1)}, bf16[1024,1024]{1,0:T(8,128)(2,1)}, u32[]{:S(2)}) copy-start(bf16[1024,1024]{1,0:T(8,128)(2,1)} %param.20) | copy-start | bytes 6291460
  16.2 724.2 %reduce-scatter.7.cloned.1.call-start = ((), (), s32[]{:S(2)}) async-start(), calls=%async_computation.8 | async-start | bytes 18874368 | tf_op jit(solution)/shard_map/reduce_scatter | solution.py:165
  49.2 89.5 %copy-start.37 = (bf16[1024,1024]{1,0:T(8,128)(2,1)S(1)}, bf16[1024,1024]{1,0:T(8,128)(2,1)}, u32[]{:S(2)}) copy-start(bf16[1024,1024]{1,0:T(8,128)(2,1)} %param.19) | copy-start | bytes 6291460
  54.0 154.6 %copy-start.10 = (pred[512,1024]{1,0:T(8,128)(4,1)}, pred[512,1024]{1,0:T(8,128)(4,1)S(1)}, u32[]{:S(2)}) copy-start(pred[512,1024]{1,0:T(8,128)(4,1)S(1)} %get-tuple-element.108) | copy-start | bytes 1572868
  54.0 193.1 %copy-start.12 = (pred[512,1024]{1,0:T(8,128)(4,1)}, pred[512,1024]{1,0:T(8,128)(4,1)S(1)}, u32[]{:S(2)}) copy-start(pred[512,1024]{1,0:T(8,128)(4,1)S(1)} %get-tuple-element.109) | copy-start | bytes 1572868
  152.7 64.9 %copy-start.4 = (bf16[1,1024,1024]{1,2,0:T(8,128)(2,1)}, bf16[1,1024,1024]{1,2,0:T(8,128)(2,1)S(1)}, u32[]{:S(2)}) copy-start(bf16[1,1024,1024]{1,2,0:T(8,128)(2,1)S(1)} %slice.220) | copy-start | bytes 6291460
  158.2 59.4 %copy-start.16 = (bf16[1,1024,16,64]{1,3,2,0:T(8,128)(2,1)}, bf16[1,1024,16,64]{1,3,2,0:T(8,128)(2,1)S(1)}, u32[]{:S(2)}) copy-start(bf16[1,1024,16,64]{1,3,2,0:T(8,128)(2,1)S(1)} %multiply_convert_fusion.5) | copy-start | bytes 6291460
  166.6 80.5 %copy-start.58 = (f32[8,512]{1,0:T(8,128)}, f32[8,512]{1,0:T(8,128)S(1)}, u32[]{:S(2)}) copy-start(f32[8,512]{1,0:T(8,128)S(1)} %get-tuple-element.112) | copy-start | bytes 49156
  175.0 33.6 %copy-start.60 = (f32[8,512]{1,0:T(8,128)}, f32[8,512]{1,0:T(8,128)S(1)}, u32[]{:S(2)}) copy-start(f32[8,512]{1,0:T(8,128)S(1)} %get-tuple-element.115) | copy-start | bytes 49156
  264.1 125.4 %copy-start.94 = (f32[1,1024]{1,0:T(1,128)S(1)}, f32[1,1024]{1,0:T(1,128)}, u32[]{:S(2)}) copy-start(f32[1,1024]{1,0:T(1,128)} %get-tuple-element.99) | copy-start | bytes 12292
  414.7 24.3 %copy-start.7 = (f32[1024,1024]{0,1:T(8,128)S(1)}, f32[1024,1024]{0,1:T(8,128)}, u32[]{:S(2)}) copy-start(f32[1024,1024]{0,1:T(8,128)} %copy-done.6) | copy-start | bytes 12582916
  454.0 561.5 %reduce-scatter.5.cloned.1.call-start = ((), (), s32[]{:S(2)}) async-start(), calls=%async_computation.7 | async-start | bytes 18874368 | tf_op jit(solution)/shard_map/reduce_scatter | solution.py:254
  475.2 34.4 %copy-start.50 = (f32[8,512]{1,0:T(8,128)}, f32[8,512]{1,0:T(8,128)S(1)}, u32[]{:S(2)}) copy-start(f32[8,512]{1,0:T(8,128)S(1)} %log_add_fusion.3) | copy-start | bytes 49156
  475.3 27.6 %copy-start.52 = (f32[8,512]{1,0:T(8,128)}, f32[8,512]{1,0:T(8,128)S(1)}, u32[]{:S(2)}) copy-start(f32[8,512]{1,0:T(8,128)S(1)} %log_add_fusion.2) | copy-start | bytes 49156
  566.1 24.4 %copy-start.51 = (f32[8,512]{1,0:T(8,128)S(1)}, f32[8,512]{1,0:T(8,128)}, u32[]{:S(2)}) copy-start(f32[8,512]{1,0:T(8,128)} %copy-done.50) | copy-start | bytes 49156
  566.1 24.4 %copy-start.53 = (f32[8,512]{1,0:T(8,128)S(1)}, f32[8,512]{1,0:T(8,128)}, u32[]{:S(2)}) copy-start(f32[8,512]{1,0:T(8,128)} %copy-done.52) | copy-start | bytes 49156
  566.1 24.4 %copy-start.55 = (f32[8,512]{1,0:T(8,128)S(1)}, f32[8,512]{1,0:T(8,128)}, u32[]{:S(2)}) copy-start(f32[8,512]{1,0:T(8,128)} %copy-done.54) | copy-start | bytes 49156
  566.1 24.4 %copy-start.57 = (f32[8,512]{1,0:T(8,128)S(1)}, f32[8,512]{1,0:T(8,128)}, u32[]{:S(2)}) copy-start(f32[8,512]{1,0:T(8,128)} %copy-done.56) | copy-start | bytes 49156
  566.1 24.4 %copy-start.68 = (f32[8,512]{1,0:T(8,128)S(1)}, f32[8,512]{1,0:T(8,128)}, u32[]{:S(2)}) copy-start(f32[8,512]{1,0:T(8,128)} %get-tuple-element.46) | copy-start | bytes 49156
  566.1 24.4 %copy-start.69 = (f32[8,512]{1,0:T(8,128)S(1)}, f32[8,512]{1,0:T(8,128)}, u32[]{:S(2)}) copy-start(f32[8,512]{1,0:T(8,128)} %get-tuple-element.47) | copy-start | bytes 49156
  708.5 590.0 %reduce-scatter.9.cloned.1.call-start = ((), (), s32[]{:S(2)}) async-start(), calls=%async_computation.9 | async-start | bytes 18874368 | tf_op jit(solution)/shard_map/reduce_scatter | solution.py:166
  724.9 630.6 %reduce-scatter.11.cloned.1.call-start = ((), (), s32[]{:S(2)}) async-start(), calls=%async_computation.10 | async-start | bytes 73728 | tf_op jit(solution)/shard_map/reduce_scatter | solution.py:255
  740.1 275.4 %copy-start.15 = (f32[4,128,1024]{1,2,0:T(8,128)S(1)}, f32[4,128,1024]{1,2,0:T(8,128)}, u32[]{:S(2)}) copy-start(f32[4,128,1024]{1,2,0:T(8,128)} %copy-done.14) | copy-start | bytes 6291460
  740.1 686.7 %all-reduce.3.cloned.1.call-start = ((), (), s32[]{:S(2)}) async-start(), calls=%async_computation.11 | async-start | bytes 6291456 | tf_op jit(solution)/shard_map/psum | solution.py:268
  1319.4 36.2 %copy-start.67 = (f32[12,128]{1,0:T(8,128)S(1)}, f32[12,128]{1,0:T(8,128)}, u32[]{:S(2)}) copy-start(f32[12,128]{1,0:T(8,128)} %param.34) | copy-start | bytes 18436
  1319.4 36.2 %copy-start.90 = (f32[1,12,128]{2,0,1:T(1,128)S(1)}, f32[1,12,128]{2,0,1:T(1,128)}, u32[]{:S(2)}) copy-start(f32[1,12,128]{2,0,1:T(1,128)} %param.36) | copy-start | bytes 18436
  1319.4 36.2 %copy-start.91 = (f32[1,12,128]{2,0,1:T(1,128)S(1)}, f32[1,12,128]{2,0,1:T(1,128)}, u32[]{:S(2)}) copy-start(f32[1,12,128]{2,0,1:T(1,128)} %param.37) | copy-start | bytes 18436
  1319.4 44.0 %copy-start.89 = (f32[12,128]{1,0:T(8,128)S(1)}, f32[12,128]{1,0:T(8,128)}, u32[]{:S(2)}) copy-start(f32[12,128]{1,0:T(8,128)} %param.35) | copy-start | bytes 18436
  (84 other events, 731.8 us)
Sparse Core Ops, SparseCore 0:
  10.6 128.0 all-gather.3
  141.4 122.6 all-gather.5
  266.8 122.6 all-gather.7
  454.1 278.3 reduce-scatter.6
  736.1 279.3 reduce-scatter.4
  1019.1 279.3 reduce-scatter.8
  1301.6 53.9 reduce-scatter.10
  1359.3 67.5 all-reduce.2
where the time goes:
time: 1480 us; the launch traced here: 1470 us
  waiting for transfers between devices  796 us (54%)
  matrix products  386 us (26%)
  other arithmetic  150 us (10%)
  local copies, waits for them, and re-layouts  82.1 us (6%)
  blocking collectives  34.9 us (2%)
  between operations  16 us (1%)
    reduce_scatter x1, waiting for transfers between devices, per_device(): lax.psum_scatter(contract_full, 'fsdp', scatter_dimension=0, tiled=True)  277 us
    reduce_scatter x1, waiting for transfers between devices, per_device(): lax.psum_scatter(grad_attention_full, 'fsdp', scatter_dimension=1, tiled=...  267 us
    all_gather x1, waiting for transfers between devices, per_device(): lax.all_gather(attention_weight.astype(jnp.bfloat16), 'fsdp', axis=1, til...  84.8 us
    all_gather x1, waiting for transfers between devices, per_device(): lax.all_gather(contract_weight.astype(jnp.bfloat16), 'fsdp', axis=0, tile...  77.4 us
    dot_general x4, matrix products, per_device(): jnp.einsum('qhd,khd->hqk', ctx_grad, value_block, preferred_element_type=...  64.3 us
    unnamed x230, local copies, waits for them, and re-layouts  62 us
    psum x1, waiting for transfers between devices, per_device(): lax.psum((attention_weight - attention_new[0]).astype(jnp.bfloat16), 'rep')  56.4 us
    convert_element_type x1, other arithmetic, per_device(): score_grad = (probability * (prob_grad - row_dot)).astype(jnp.bfloat16)  52.7 us
  transfers between devices with their start and end apart: 8, of which 7 were waited for; matrix products, arithmetic and copies ran while one was open for 34% of the time, Pallas kernels for 0%

commit v1 on v0

--- a/solution.py
+++ b/solution.py
@@ -1,3 +1,4 @@
+import functools
 from functools import partial
 import jax
 import jax.numpy as jnp
@@ -12,6 +13,28 @@
 SEQ_DEV = 1
 ADAM_STEP = 4
 TOK_DEV = 1024
+
+
+def put_turns(inputs, chip_axis):
+    answer, tmp, local_now = (lax.axis_size(chip_axis), lax.axis_index(chip_axis), inputs.shape[1])
+    pieces_in = [(k, (k + 1) % answer) for k in range(answer)]
+    grid = [(k, (k - 1) % answer) for k in range(answer)]
+    r2 = jnp.zeros((*inputs.shape[:1], answer * local_now, *inputs.shape[2:]), inputs.dtype)
+    everything = right_arr = inputs
+    r2 = lax.dynamic_update_slice_in_dim(r2, inputs, tmp * local_now, axis=1)
+    top = answer // 2
+    for d in range(1, top + 1):
+        everything = lax.ppermute(everything, chip_axis, pieces_in)
+        r2 = lax.dynamic_update_slice_in_dim(r2, everything, (tmp - d) % answer * local_now, axis=1)
+        if d < answer - top:
+            right_arr = lax.ppermute(right_arr, chip_axis, grid)
+            r2 = lax.dynamic_update_slice_in_dim(
+                r2, right_arr, (tmp + d) % answer * local_now, axis=1
+            )
+    return r2
+
+
+time_slots = functools.partial(put_turns, chip_axis="fsdp")
 
 
 def norm_forward(values_in, gain_row, shift_row):
@@ -84,7 +107,7 @@
     vectors_second,
 ):
     attn_full, vector_full = (
-        lax.all_gather(attention_weight.astype(jnp.bfloat16), "fsdp", axis=1, tiled=True),
+        time_slots(attention_weight.astype(jnp.bfloat16)),
         lax.all_gather(vectors.astype(jnp.bfloat16), "fsdp", axis=1, tiled=True),
     )
     vector_rows = vector_full.astype(jnp.float32)

time: 1480 us -> 1520 us (1.027)
  blocking collectives: 34.9 us -> 70.4 us
  waiting for transfers between devices: 796 us -> 775 us
  starting transfers between devices: 0.58 us -> 20.1 us
  local copies, waits for them, and re-layouts: 82.1 us -> 97.9 us
    ppermute x0 -> x7, waiting for transfers between devices: none -> 143 us  [the longest x4 127 us: put_turns(): everything = lax.ppermute(everything, chip_axis, pieces_in)]
    all_gather x1 -> x0, waiting for transfers between devices: 84.8 us -> none  [per_device(): lax.all_gather(attention_weight.astype(jnp.bfloat16), 'fsdp', axis=1, til...]
    all_gather x1, waiting for transfers between devices: 77.4 us -> 0.01 us  [per_device(): lax.all_gather(contract_weight.astype(jnp.bfloat16), 'fsdp', axis=0, tile...]
    all_gather x1, blocking collectives: 28.9 us -> 64.6 us  [per_device(): lax.all_gather(vectors.astype(jnp.bfloat16), 'fsdp', axis=1, tiled=True)]
    ppermute x0 -> x7, starting transfers between devices: none -> 19.4 us  [the longest x3 10.6 us: put_turns(): right_arr = lax.ppermute(right_arr, chip_axis, grid)]
    unnamed x230 -> x236, local copies, waits for them, and re-layouts: 62 us -> 62.5 us
  transfers between devices with their start and end apart: 8 -> 14, of which waited for: 7 -> 8; matrix products, arithmetic and copies ran while one was open for 34% -> 34% of each run, Pallas kernels for 0% -> 0%
where the time goes in v1:
time: 1520 us
  waiting for transfers between devices  775 us (51%)
  matrix products  390 us (26%)
  other arithmetic  148 us (10%)
  local copies, waits for them, and re-layouts  97.9 us (6%)
  blocking collectives  70.4 us (5%)
  starting transfers between devices  20.1 us (1%)
  between operations  15.7 us (1%)
    reduce_scatter x1, waiting for transfers between devices, per_device(): lax.psum_scatter(contract_full, 'fsdp', scatter_dimension=0, tiled=True)  277 us
    reduce_scatter x1, waiting for transfers between devices, per_device(): lax.psum_scatter(grad_attention_full, 'fsdp', scatter_dimension=1, tiled=...  266 us
    ppermute x4, waiting for transfers between devices, put_turns(): everything = lax.ppermute(everything, chip_axis, pieces_in)  127 us
    all_gather x1, blocking collectives, per_device(): lax.all_gather(vectors.astype(jnp.bfloat16), 'fsdp', axis=1, tiled=True)  64.6 us
    dot_general x4, matrix products, per_device(): jnp.einsum('qhd,khd->hqk', ctx_grad, value_block, preferred_element_type=...  64.3 us
    unnamed x236, local copies, waits for them, and re-layouts  62.5 us
    psum x1, waiting for transfers between devices, per_device(): lax.psum((attention_weight - attention_new[0]).astype(jnp.bfloat16), 'rep')  56.5 us
    convert_element_type x1, other arithmetic, per_device(): score_grad = (probability * (prob_grad - row_dot)).astype(jnp.bfloat16)  52.8 us
  transfers between devices with their start and end apart: 14, of which 8 were waited for; matrix products, arithmetic and copies ran while one was open for 34% of the time, Pallas kernels for 0%

profile of v1, /device:TPU:0, one launch (start us, length us, event | category | flops | bytes accessed | tf_op | source)
XLA Modules:
  0.0 1516.4 jit_solution(11535919195929365812)
XLA Ops:
  23.1 53.1 %collective-permute-done = bf16[4,128,1024]{1,2,0:T(8,128)(2,1)S(1)} collective-permute-done((bf16[4,128,1024]{1,2,0:T(8,128)(2,1)S(1)}, bf16[4,128,1024]{1,2,0:T(8,128)(2,1)S(1)}, u32[]{:S(2)}, u32[]{:S(2)}) %collective-permute-start) | collective-permute-done | bytes 1048608 | tf_op jit(solution)/shard_map/ppermute | solution.py:27
  82.7 60.0 %collective-permute-done.2 = bf16[4,128,1024]{1,2,0:T(8,128)(2,1)} collective-permute-done((bf16[4,128,1024]{1,2,0:T(8,128)(2,1)S(1)}, bf16[4,128,1024]{1,2,0:T(8,128)(2,1)}, u32[]{:S(2)}, u32[]{:S(2)}) %collective-permute-start.2) | collective-permute-done | bytes 1048608 | tf_op jit(solution)/shard_map/ppermute | solution.py:27
  147.0 64.6 %all_gather.9 = bf16[12,1024]{1,0:T(8,128)(2,1)S(1)} all-gather(bf16[12,128]{1,0:T(8,128)(2,1)S(1)} %convert_element_type.221), channel_id=1, replica_groups=mesh['rep'=4,'fsdp'=8] {'fsdp'}, dimensions={1}, use_global_device_ids=true | all-gather | bytes 27648 | tf_op jit(solution)/shard_map/all_gather | solution.py:111
  234.8 15.5 %collective-permute-done.5 = bf16[4,128,1024]{1,2,0:T(8,128)(2,1)} collective-permute-done((bf16[4,128,1024]{1,2,0:T(8,128)(2,1)}, bf16[4,128,1024]{1,2,0:T(8,128)(2,1)}, u32[]{:S(2)}, u32[]{:S(2)}) %collective-permute-start.5) | collective-permute-done | bytes 1048608 | tf_op jit(solution)/shard_map/ppermute | solution.py:30
  252.8 14.1 collective-permute-done.6
  268.0 9.0 convolution_bitcast_fusion.1
  287.4 9.2 select_reduce_fusion.1
  296.6 8.4 select_reduce_fusion.3
  306.6 13.8 fusion.6
  338.0 9.3 fusion.78
  347.3 13.5 fusion.8
  376.4 8.3 fusion.76
  391.9 48.2 %multiply_convert_fusion.4 = (bf16[1024,4096]{1,0:T(8,128)(2,1)}, f32[1024,4096]{1,0:T(8,128)}, f32[1024,4096]{1,0:T(8,128)}) fusion(f32[4096]{0:T(1024)S(1)} %bitcast.308, bf16[1024,4096]{1,0:T(8,128)(2,1)} %all-gather.3.cloned.1.call-done, bf16[1024,1024]{0,1:T(8,128)(2,1)S(1)} %fusion.134.clone.4), kind=kOutput, calls=%fused_computation.17 | convolution fusion | flops 8866758656 | bytes 52445184 | tf_op jit(solution)/shard_map/dot_general | solution.py:173
  440.1 14.9 fusion.141
  465.4 24.3 %convert_reduce_fusion = (f32[4096]{0:T(1024)}, bf16[1024,4096]{1,0:T(8,128)(2,1)}) fusion(f32[1024,4096]{1,0:T(8,128)} %get-tuple-element.66, f32[1024,4096]{1,0:T(8,128)} %get-tuple-element.122, f32[4096]{0:T(1024)S(1)} %bitcast.309, bf16[1024,1024]{0,1:T(8,128)(2,1)} %get-tuple-element.60, bf16[4096,1024]{1,0:T(8,128)(2,1)} %all-gather.5.cloned.1.call-done), kind=kOutput, calls=%fused_computation.3 | convolution fusion | flops 8661233664 | bytes 52461568 | tf_op jit(solution)/shard_map/dot_general | solution.py:66
  489.8 14.9 fusion.131
  509.2 18.2 %multiply_reduce_fusion.4 = (f32[1024]{0:T(1024)}, f32[1024]{0:T(1024)S(1)}, f32[1024]{0:T(1024)S(1)}, f32[1024]{0:T(1024)}, f32[1024,1024]{0,1:T(8,128)S(1)}) fusion(f32[1024,1024]{0,1:T(8,128)S(1)} %copy-done.8, f32[1024]{0:T(1024)S(1)} %add_rsqrt_fusion.1, f32[1024]{0:T(1024)S(1)} %broadcast_multiply_fusion.5, f32[1024]{0:T(1024)S(1)} %bitcast.296, ...), kind=kOutput, calls=%fused_computation.96 | convolution fusion | flops 8608804864 | bytes 31506432 | tf_op jit(solution)/shard_map/dot_general | solution.py:66
  535.1 10.1 fusion.14
  545.2 9.9 fusion.16
  561.9 10.6 fusion.81
  578.4 9.4 fusion.95
  587.9 9.3 fusion.96
  597.2 21.2 %multiply_reduce_fusion.3 = (f32[8,512]{1,0:T(8,128)}, f32[8,512]{1,0:T(8,128)}, f32[8,512,1024]{2,1,0:T(8,128)}) fusion(f32[8,512,1024]{2,1,0:T(8,128)} %get-tuple-element.118, f32[8,512]{1,0:T(8,128)} %copy-done.53, pred[512,1024]{1,0:T(8,128)(4,1)S(1)} %copy-done.11, f32[8,512,1024]{2,1,0:T(8,128)} %fusion.96, f32[8,512]{1,0:T(8,128)} %copy-done.55, ...), kind=kOutput, calls=%fused_computation.14 | convolution fusion | flops 570417152 | bytes 69271552 | tf_op jit(solution)/shard_map/qhd,khd->hqk/dot_general | solution.py:230
  618.4 24.4 %multiply_reduce_fusion.1 = (f32[8,512]{1,0:T(8,128)S(1)}, f32[8,512]{1,0:T(8,128)S(1)}, f32[8,512,1024]{2,1,0:T(8,128)}) fusion(f32[8,512,1024]{2,1,0:T(8,128)} %get-tuple-element.115, f32[8,512]{1,0:T(8,128)} %copy-done.57, pred[512,1024]{1,0:T(8,128)(4,1)S(1)} %copy-done.13, f32[8,512,1024]{2,1,0:T(8,128)} %fusion.95, f32[8,512]{1,0:T(8,128)} %copy-done.59, ...), kind=kOutput, calls=%fused_computation.8 | convolution fusion | flops 570417152 | bytes 69271552 | tf_op jit(solution)/shard_map/qhd,khd->hqk/dot_general | solution.py:230
  642.8 52.8 %multiply_convert_fusion.1 = (bf16[8,512,1024]{2,1,0:T(8,128)(2,1)}, bf16[8,512,1024]{2,1,0:T(8,128)(2,1)S(1)}, bf16[8,512,1024]{2,1,0:T(8,128)(2,1)}, bf16[8,512,1024]{2,1,0:T(8,128)(2,1)}) fusion(f32[8,512,1024]{2,1,0:T(8,128)} %get-tuple-element.127, f32[8,512,1024]{2,1,0:T(8,128)} %get-tuple-element.115, f32[8,512]{1,0:T(8,128)S(1)} %get-tuple-element.44, ...), kind=kLoop, calls=%fused_computation.7 | loop fusion | flops 83886080 | bytes 168951808 | tf_op jit(solution)/shard_map/convert_element_type | solution.py:234
  761.4 14.9 fusion.142
  792.0 8.4 fusion.100
  800.4 266.5 %reduce-scatter.5.cloned.1.call-done = f32[4,128,1024]{1,2,0:T(8,128)} async-done(((f32[4,1024,1024]{1,2,0:T(8,128)}), f32[4,128,1024]{1,2,0:T(8,128)}) %reduce-scatter.5.cloned.1.call-update) | async-done | bytes 2097168 | tf_op jit(solution)/shard_map/reduce_scatter | solution.py:277
  1073.0 276.9 %reduce-scatter.9.cloned.1.call-done = f32[512,1024]{1,0:T(8,128)} async-done(((f32[4096,1024]{1,0:T(8,128)}), f32[512,1024]{1,0:T(8,128)}) %reduce-scatter.9.cloned.1.call-update) | async-done | bytes 2097168 | tf_op jit(solution)/shard_map/reduce_scatter | solution.py:189
  1357.8 12.9 fusion.47
  1374.7 32.1 %reduce-scatter.11.cloned.1.call-done = f32[12,128]{1,0:T(8,128)} async-done(((f32[12,1024]{1,0:T(8,128)}), f32[12,128]{1,0:T(8,128)}) %reduce-scatter.11.cloned.1.call-update) | async-done | bytes 6160 | tf_op jit(solution)/shard_map/reduce_scatter | solution.py:278
  1421.6 56.5 %all-reduce.3.cloned.1.call-done = (bf16[4,128,1024]{1,2,0:T(8,128)(2,1)}, bf16[128,4096]{1,0:T(8,128)(2,1)}, bf16[512,1024]{1,0:T(8,128)(2,1)}) async-done(((bf16[4,128,1024]{1,2,0:T(8,128)(2,1)}, bf16[128,4096]{1,0:T(8,128)(2,1)}, bf16[512,1024]{1,0:T(8,128)(2,1)}), (bf16[4,128,1024]{1,2,0:T(8,128)(2,1)}, bf16[128,4096]{1,0:T(8,128)(2,1)}, bf16[512,1024]{1,0:T(8,128)(2,1)})) %all-reduce.3.cloned.1.call-update) | async-done | bytes 3145744 | tf_op jit(solution)/shard_map/psum | solution.py:291
  (354 shorter events, 285.8 us)
Async XLA Ops:
  7.2 384.7 %all-gather.3.cloned.1.call-start = ((), (), s32[]{:S(2)}) async-start(), calls=%async_computation.4 | async-start | bytes 9437184 | tf_op jit(solution)/shard_map/all_gather | solution.py:170
  10.0 430.2 %all-gather.5.cloned.1.call-start = ((), (), s32[]{:S(2)}) async-start(), calls=%async_computation.5 | async-start | bytes 9437184 | tf_op jit(solution)/shard_map/all_gather | solution.py:171
  13.2 132.5 %copy-start.24 = (f32[512,1024]{1,0:T(8,128)S(1)}, f32[512,1024]{1,0:T(8,128)}, u32[]{:S(2)}) copy-start(f32[512,1024]{1,0:T(8,128)} %param.30) | copy-start | bytes 6291460
  13.2 133.7 %copy-start.69 = (f32[12,128]{1,0:T(8,128)S(1)}, f32[12,128]{1,0:T(8,128)}, u32[]{:S(2)}) copy-start(f32[12,128]{1,0:T(8,128)} %param.34) | copy-start | bytes 18436
  13.2 198.3 %copy-start.87 = (s32[1,1024]{1,0:T(1,128)S(1)}, s32[1,1024]{1,0:T(1,128)}, u32[]{:S(2)}) copy-start(s32[1,1024]{1,0:T(1,128)} %param.21) | copy-start | bytes 12292
  17.1 199.5 %copy-start.37 = (bf16[1024,1024]{1,0:T(8,128)(2,1)S(1)}, bf16[1024,1024]{1,0:T(8,128)(2,1)}, u32[]{:S(2)}) copy-start(bf16[1024,1024]{1,0:T(8,128)(2,1)} %param.20) | copy-start | bytes 6291460
  17.1 59.1 %collective-permute-start = (bf16[4,128,1024]{1,2,0:T(8,128)(2,1)S(1)}, bf16[4,128,1024]{1,2,0:T(8,128)(2,1)S(1)}, u32[]{:S(2)}, u32[]{:S(2)}) collective-permute-start(bf16[4,128,1024]{1,2,0:T(8,128)(2,1)S(1)} %get-tuple-element.68), channel_id=1, source_target_pairs={{0,1},{1,2},{2,3},{3,4},{4,5},{5,6},{6,7},{7,0},{8,9},{9,10},{10,1... | collective-permute-start | bytes 3145736 | tf_op jit(solution)/shard_map/ppermute | solution.py:27
  20.1 58.6 %collective-permute-start.1 = (bf16[4,128,1024]{1,2,0:T(8,128)(2,1)S(1)}, bf16[4,128,1024]{1,2,0:T(8,128)(2,1)}, u32[]{:S(2)}, u32[]{:S(2)}) collective-permute-start(bf16[4,128,1024]{1,2,0:T(8,128)(2,1)S(1)} %get-tuple-element.68), channel_id=1, source_target_pairs={{0,7},{1,0},{2,1},{3,2},{4,3},{5,4},{6,5},{7,6},{8,15},{9,8},{10,9... | collective-permute-start | bytes 3145736 | tf_op jit(solution)/shard_map/ppermute | solution.py:30
  76.2 66.5 %collective-permute-start.2 = (bf16[4,128,1024]{1,2,0:T(8,128)(2,1)S(1)}, bf16[4,128,1024]{1,2,0:T(8,128)(2,1)}, u32[]{:S(2)}, u32[]{:S(2)}) collective-permute-start(bf16[4,128,1024]{1,2,0:T(8,128)(2,1)S(1)} %collective-permute-done), channel_id=1, source_target_pairs={{0,1},{1,2},{2,3},{3,4},{4,5},{5,6},{6,7},{7,0},{8,9},{9,10},{10,1... | collective-permute-start | bytes 3145736 | tf_op jit(solution)/shard_map/ppermute | solution.py:27
  78.7 133.6 %collective-permute-start.3 = (bf16[4,128,1024]{1,2,0:T(8,128)(2,1)}, bf16[4,128,1024]{1,2,0:T(8,128)(2,1)}, u32[]{:S(2)}, u32[]{:S(2)}) collective-permute-start(bf16[4,128,1024]{1,2,0:T(8,128)(2,1)} %collective-permute-done.1), channel_id=1, source_target_pairs={{0,7},{1,0},{2,1},{3,2},{4,3},{5,4},{6,5},{7,6},{8,15},{9,8},{10,9... | collective-permute-start | bytes 3145736 | tf_op jit(solution)/shard_map/ppermute | solution.py:30
  142.7 80.5 %collective-permute-start.4 = (bf16[4,128,1024]{1,2,0:T(8,128)(2,1)}, bf16[4,128,1024]{1,2,0:T(8,128)(2,1)}, u32[]{:S(2)}, u32[]{:S(2)}) collective-permute-start(bf16[4,128,1024]{1,2,0:T(8,128)(2,1)} %collective-permute-done.2), channel_id=1, source_target_pairs={{0,1},{1,2},{2,3},{3,4},{4,5},{5,6},{6,7},{7,0},{8,9},{9,10},{10,1... | collective-permute-start | bytes 3145736 | tf_op jit(solution)/shard_map/ppermute | solution.py:27
  146.9 645.1 %reduce-scatter.7.cloned.1.call-start = ((), (), s32[]{:S(2)}) async-start(), calls=%async_computation.7 | async-start | bytes 18874368 | tf_op jit(solution)/shard_map/reduce_scatter | solution.py:188
  212.2 125.7 %copy-start.10 = (pred[512,1024]{1,0:T(8,128)(4,1)}, pred[512,1024]{1,0:T(8,128)(4,1)S(1)}, u32[]{:S(2)}) copy-start(pred[512,1024]{1,0:T(8,128)(4,1)S(1)} %get-tuple-element.110) | copy-start | bytes 1572868
  212.2 164.1 %copy-start.12 = (pred[512,1024]{1,0:T(8,128)(4,1)}, pred[512,1024]{1,0:T(8,128)(4,1)S(1)}, u32[]{:S(2)}) copy-start(pred[512,1024]{1,0:T(8,128)(4,1)S(1)} %get-tuple-element.111) | copy-start | bytes 1572868
  212.3 38.1 %collective-permute-start.5 = (bf16[4,128,1024]{1,2,0:T(8,128)(2,1)}, bf16[4,128,1024]{1,2,0:T(8,128)(2,1)}, u32[]{:S(2)}, u32[]{:S(2)}) collective-permute-start(bf16[4,128,1024]{1,2,0:T(8,128)(2,1)} %collective-permute-done.3), channel_id=1, source_target_pairs={{0,7},{1,0},{2,1},{3,2},{4,3},{5,4},{6,5},{7,6},{8,15},{9,8},{10,9... | collective-permute-start | bytes 3145736 | tf_op jit(solution)/shard_map/ppermute | solution.py:30
  223.1 43.7 %collective-permute-start.6 = (bf16[4,128,1024]{1,2,0:T(8,128)(2,1)}, bf16[4,128,1024]{1,2,0:T(8,128)(2,1)S(1)}, u32[]{:S(2)}, u32[]{:S(2)}) collective-permute-start(bf16[4,128,1024]{1,2,0:T(8,128)(2,1)} %collective-permute-done.4), channel_id=1, source_target_pairs={{0,1},{1,2},{2,3},{3,4},{4,5},{5,6},{6,7},{7,0},{8,9},{9,10},{10,1... | collective-permute-start | bytes 3145736 | tf_op jit(solution)/shard_map/ppermute | solution.py:27
  229.9 38.1 %copy-start.38 = (bf16[1024,1024]{1,0:T(8,128)(2,1)S(1)}, bf16[1024,1024]{1,0:T(8,128)(2,1)}, u32[]{:S(2)}) copy-start(bf16[1024,1024]{1,0:T(8,128)(2,1)} %param.19) | copy-start | bytes 6291460
  281.9 65.3 %copy-start.4 = (bf16[1,1024,1024]{1,2,0:T(8,128)(2,1)}, bf16[1,1024,1024]{1,2,0:T(8,128)(2,1)S(1)}, u32[]{:S(2)}) copy-start(bf16[1,1024,1024]{1,2,0:T(8,128)(2,1)S(1)} %slice.220) | copy-start | bytes 6291460
  287.4 59.9 %copy-start.16 = (bf16[1,1024,16,64]{1,3,2,0:T(8,128)(2,1)}, bf16[1,1024,16,64]{1,3,2,0:T(8,128)(2,1)S(1)}, u32[]{:S(2)}) copy-start(bf16[1,1024,16,64]{1,3,2,0:T(8,128)(2,1)S(1)} %multiply_convert_fusion.5) | copy-start | bytes 6291460
  296.6 79.7 %copy-start.61 = (f32[8,512]{1,0:T(8,128)}, f32[8,512]{1,0:T(8,128)S(1)}, u32[]{:S(2)}) copy-start(f32[8,512]{1,0:T(8,128)S(1)} %get-tuple-element.114) | copy-start | bytes 49156
  391.9 48.2 %copy-start.97 = (f32[1,1024]{1,0:T(1,128)S(1)}, f32[1,1024]{1,0:T(1,128)}, u32[]{:S(2)}) copy-start(f32[1,1024]{1,0:T(1,128)} %get-tuple-element.101) | copy-start | bytes 12292
  504.8 562.1 %reduce-scatter.5.cloned.1.call-start = ((), (), s32[]{:S(2)}) async-start(), calls=%async_computation.6 | async-start | bytes 18874368 | tf_op jit(solution)/shard_map/reduce_scatter | solution.py:277
  509.1 52.8 %copy-start.53 = (f32[8,512]{1,0:T(8,128)}, f32[8,512]{1,0:T(8,128)S(1)}, u32[]{:S(2)}) copy-start(f32[8,512]{1,0:T(8,128)S(1)} %log_add_fusion.3) | copy-start | bytes 49156
  509.1 46.0 %copy-start.55 = (f32[8,512]{1,0:T(8,128)}, f32[8,512]{1,0:T(8,128)S(1)}, u32[]{:S(2)}) copy-start(f32[8,512]{1,0:T(8,128)S(1)} %log_add_fusion.2) | copy-start | bytes 49156
  759.8 590.1 %reduce-scatter.9.cloned.1.call-start = ((), (), s32[]{:S(2)}) async-start(), calls=%async_computation.8 | async-start | bytes 18874368 | tf_op jit(solution)/shard_map/reduce_scatter | solution.py:189
  776.3 630.5 %reduce-scatter.11.cloned.1.call-start = ((), (), s32[]{:S(2)}) async-start(), calls=%async_computation.9 | async-start | bytes 73728 | tf_op jit(solution)/shard_map/reduce_scatter | solution.py:278
  791.5 275.4 %copy-start.15 = (f32[4,128,1024]{1,2,0:T(8,128)S(1)}, f32[4,128,1024]{1,2,0:T(8,128)}, u32[]{:S(2)}) copy-start(f32[4,128,1024]{1,2,0:T(8,128)} %copy-done.14) | copy-start | bytes 6291460
  791.5 686.6 %all-reduce.3.cloned.1.call-start = ((), (), s32[]{:S(2)}) async-start(), calls=%async_computation.10 | async-start | bytes 6291456 | tf_op jit(solution)/shard_map/psum | solution.py:291
  1370.7 36.1 %copy-start.70 = (f32[12,128]{1,0:T(8,128)S(1)}, f32[12,128]{1,0:T(8,128)}, u32[]{:S(2)}) copy-start(f32[12,128]{1,0:T(8,128)} %param.34) | copy-start | bytes 18436
  1370.7 36.2 %copy-start.93 = (f32[1,12,128]{2,0,1:T(1,128)S(1)}, f32[1,12,128]{2,0,1:T(1,128)}, u32[]{:S(2)}) copy-start(f32[1,12,128]{2,0,1:T(1,128)} %param.36) | copy-start | bytes 18436
  1370.7 36.1 %copy-start.94 = (f32[1,12,128]{2,0,1:T(1,128)S(1)}, f32[1,12,128]{2,0,1:T(1,128)}, u32[]{:S(2)}) copy-start(f32[1,12,128]{2,0,1:T(1,128)} %param.37) | copy-start | bytes 18436
  1370.7 43.9 %copy-start.92 = (f32[12,128]{1,0:T(8,128)S(1)}, f32[12,128]{1,0:T(8,128)}, u32[]{:S(2)}) copy-start(f32[12,128]{1,0:T(8,128)} %param.35) | copy-start | bytes 18436
  (93 other events, 825.8 us)
Sparse Core Ops, SparseCore 0:
  10.7 213.3 all-gather.2
  226.8 140.9 all-gather.4
  504.8 278.9 reduce-scatter.6
  787.5 279.3 reduce-scatter.4
  1070.5 279.3 reduce-scatter.8
  1352.9 53.9 reduce-scatter.10
  1410.5 67.4 all-reduce.2
